TPU v7x, 32 devices: a whole 2x2x4 slice. The times are simulated.
32 devices in a mesh: copy: 2 (over core), fsdp: 4 (over z), tp: 4 (over y, x).
Axes of the slice: x: 2, y: 2, z: 4, core: 2. Of those that a mesh axis runs over, the one named last changes fastest.
Arguments:
- gradients: float32 [32, 128, 4096], P('copy', 'fsdp', 'tp'), parts along dimension 0, may hold values from -6 to 6
- momentum: float32 [32, 128, 4096], P('copy', 'fsdp', 'tp'), parts along dimension 0, may hold values from -6 to 6
- weights: float32 [32, 128, 4096], P('copy', 'fsdp', 'tp'), parts along dimension 0, may hold values from -0.1875 to 0.1875
Outputs:
- new_weights: float32 [32, 128, 4096], P('copy', 'fsdp', 'tp'), parts along dimension 0
- new_momentum: float32 [32, 128, 4096], P('copy', 'fsdp', 'tp'), parts along dimension 0
There are 2 independent parts, one for each index of `copy`. A program takes and returns all parts, laid end to end along the dimension named above; each array names one. Nothing has to cross between parts.
All inputs are finite; a program needn't handle non-finite values.
Results may differ from a plain program's by a relative error of at most 0.00014.
Values sent between devices are 32-bit elements; how exact they have to be, the bound alone decides.
A program may use at most 64 MiB of HBM per device.

v0:
```python
import jax
import jax.numpy as jnp
from jax import lax
from jax.sharding import PartitionSpec as P

ITERS = 4
hold_rate = 0.95
learn_rate = 0.9
decay_rate = 0.1


def mul(a, b):
    return jnp.einsum("mij,mjk->mik", a, b, precision=lax.Precision.HIGHEST)


def mixing(gram):
    eye = jnp.eye(gram.shape[-1], dtype=gram.dtype)
    scale = lax.rsqrt(jnp.sum(gram * eye, axis=(1, 2), keepdims=True) + 1e-06)
    gram = gram * scale * scale
    total = scale * eye
    for step in range(ITERS):
        poly = 3.4445 * eye - 4.775 * gram + 2.0315 * mul(gram, gram)
        total = mul(poly, total)
        if step < ITERS - 1:
            gram = mul(poly, mul(gram, poly))
    return total


def shards(gradients, momentum, weights):
    new_momentum = hold_rate * momentum + gradients
    direction = hold_rate * new_momentum + gradients
    moved = lax.all_to_all(direction, "fsdp", split_axis=0, concat_axis=1, tiled=True)
    gram = jnp.einsum("mik,mjk->mij", moved, moved, precision=lax.Precision.HIGHEST)
    gram = lax.psum(gram, "tp")
    iterate = mul(mixing(gram), moved)
    back = lax.all_to_all(iterate, "fsdp", split_axis=1, concat_axis=0, tiled=True)
    new_weights = (1.0 - learn_rate * decay_rate) * weights - learn_rate * back
    return (new_weights, new_momentum)


def solution(mesh):
    return jax.shard_map(
        shards,
        mesh=mesh,
        in_specs=(P("copy", "fsdp", "tp"), P("copy", "fsdp", "tp"), P("copy", "fsdp", "tp")),
        out_specs=(P("copy", "fsdp", "tp"), P("copy", "fsdp", "tp")),
        check_vma=False,
    )
```

profile of v0, /device:TPU:0, one launch (start us, length us, event | category | flops | bytes accessed | tf_op | source)
XLA Modules:
  0.0 186.5 jit_solution(14155956798188366832)
XLA Ops:
  7.2 0.0 all-reduce.2.cloned.1.call-start
  7.2 4.5 %multiply_add_fusion = (f32[16,32,1024]{2,1,0:T(8,128)S(1)}, f32[16,32,1024]{2,1,0:T(8,128)}) fusion(f32[16,32,1024]{2,1,0:T(8,128)} %param.3, f32[16,32,1024]{2,1,0:T(8,128)} %param.4), kind=kLoop, calls=%fused_computation.1 | loop fusion | flops 2097152 | bytes 8388608 | tf_op jit(solution)/shard_map/add | solution.py:31
  11.7 54.3 %all_to_all.27 = f32[16,32,1024]{2,1,0:T(8,128)S(1)} all-to-all(f32[16,32,1024]{2,1,0:T(8,128)S(1)} %get-tuple-element.2), channel_id=1, replica_groups=mesh['copy'=2,'fsdp'=4,'tp'=4] {'fsdp'}, dimensions={0} | all-to-all | bytes 4194304 | tf_op jit(solution)/shard_map/all_to_all | solution.py:32
  66.0 0.1 copy.7
  66.2 2.8 %fusion.13 = f32[4,128,128]{2,1,0:T(8,128)} fusion(f32[4,128,1024]{2,1,0:T(8,128)S(1)} %bitcast.37), kind=kOutput, calls=%fused_computation.25 | convolution fusion | flops 805306368 | bytes 2359296 | tf_op jit(solution)/shard_map/mik,mjk->mij/dot_general | solution.py:33
  68.9 0.0 all-reduce.2.cloned.1.call-update
  69.0 42.4 %all-reduce.2.cloned.1.call-done = f32[4,128,128]{2,1,0:T(8,128)} async-done(((f32[4,128,128]{2,1,0:T(8,128)}), f32[4,128,128]{2,1,0:T(8,128)}) %all-reduce.2.cloned.1.call-update) | async-done | bytes 262160 | tf_op jit(solution)/shard_map/psum | solution.py:34
  111.4 1.1 multiply_reduce_fusion
  112.5 1.6 fusion.3
  114.1 0.4 fusion.4
  114.6 1.4 fusion.6
  116.0 0.4 fusion.14
  116.4 0.4 fusion.2
  116.7 0.4 fusion.15
  117.1 0.4 fusion.19
  117.5 0.4 fusion.16
  118.0 0.4 fusion.1
  118.3 0.4 fusion.17
  118.7 0.4 fusion.20
  119.1 0.4 fusion.18
  119.5 0.4 fusion
  119.9 0.4 fusion.21
  120.3 1.9 %fusion.22 = f32[4,128,1024]{2,1,0:T(8,128)S(1)} fusion(f32[4,128,128]{2,1,0:T(8,128)S(1)} %fusion.21, f32[4,128,1024]{2,1,0:T(8,128)S(1)} %bitcast.38), kind=kOutput, calls=%fused_computation.34 | convolution fusion | flops 805306368 | bytes 4456448 | tf_op jit(solution)/shard_map/mij,mjk->mik/dot_general | solution.py:13
  122.3 1.4 copy.8
  123.6 52.1 %all_to_all.28 = f32[4,128,1024]{2,0,1:T(4,128)S(1)} all-to-all(f32[4,128,1024]{2,0,1:T(4,128)S(1)} %copy.8), channel_id=1, replica_groups=mesh['copy'=2,'fsdp'=4,'tp'=4] {'fsdp'}, dimensions={1} | all-to-all | bytes 4194304 | tf_op jit(solution)/shard_map/all_to_all | solution.py:36
  175.7 0.6 broadcast_multiply_fusion
  176.3 0.0 copy-start
  176.3 1.2 copy.9
  177.6 0.4 copy-done
  177.9 1.8 bitcast_subtract_fusion
  (3 shorter events, 0.0 us)
Async XLA Ops:
  7.2 104.2 %all-reduce.2.cloned.1.call-start = ((), (), s32[]{:S(2)}) async-start(), calls=%async_computation.2 | async-start | bytes 524288 | tf_op jit(solution)/shard_map/psum | solution.py:34
  176.3 1.6 copy-start
Sparse Core Ops, SparseCore 0:
  69.1 42.2 all-reduce.1
where the time goes:
time: 187 us
  blocking collectives  106 us (57%)
  waiting for transfers between devices  42.4 us (23%)
  between operations  14.2 us (8%)
  matrix products  12.4 us (7%)
  other arithmetic  7.95 us (4%)
  local copies, waits for them, and re-layouts  3.07 us (2%)
    all_to_all x1, blocking collectives, shards(): lax.all_to_all(direction, 'fsdp', split_axis=0, concat_axis=1, tiled=True)  54.3 us
    all_to_all x1, blocking collectives, shards(): lax.all_to_all(iterate, 'fsdp', split_axis=1, concat_axis=0, tiled=True)  52.1 us
    psum x1, waiting for transfers between devices, shards(): gram = lax.psum(gram, 'tp')  42.4 us
    dot_general x15, matrix products, mul(): return jnp.einsum('mij,mjk->mik', a, b, precision=lax.Precision.HIGHEST)  9.65 us
    add x1, other arithmetic, shards(): direction = hold_rate * new_momentum + gradients  4.5 us
  transfers between devices with their start and end apart: 1, of which 1 were waited for; matrix products, arithmetic and copies ran while one was open for 0% of the time, Pallas kernels for 0%

commit v1 on v0

--- a/solution.py
+++ b/solution.py
@@ -31,7 +31,9 @@
     direction = hold_rate * new_momentum + gradients
     moved = lax.all_to_all(direction, "fsdp", split_axis=0, concat_axis=1, tiled=True)
     gram = jnp.einsum("mik,mjk->mij", moved, moved, precision=lax.Precision.HIGHEST)
-    gram = lax.psum(gram, "tp")
+    gram = gram
+    for hop in (1, 2):
+        gram = gram + lax.ppermute(gram, "tp", [(dev, dev ^ hop) for dev in range(4)])
     iterate = mul(mixing(gram), moved)
     back = lax.all_to_all(iterate, "fsdp", split_axis=1, concat_axis=0, tiled=True)
     new_weights = (1.0 - learn_rate * decay_rate) * weights - learn_rate * back

time: 187 us -> 138 us (0.74)
  waiting for transfers between devices: 42.4 us -> 10.3 us
  between operations: 14.2 us -> 0.81 us
  starting transfers between devices: 0.04 us -> 3.14 us
  matrix products: 12.4 us -> 9.63 us
  blocking collectives: 106 us -> 104 us
    psum x1 -> x0, waiting for transfers between devices: 42.4 us -> none  [shards(): gram = lax.psum(gram, 'tp')]
    ppermute x0 -> x2, waiting for transfers between devices: none -> 10.3 us  [shards(): lax.ppermute(gram, 'tp', [(dev, dev ^ hop) for dev in range(4)])]
    ppermute x0 -> x2, starting transfers between devices: none -> 3.14 us  [shards(): lax.ppermute(gram, 'tp', [(dev, dev ^ hop) for dev in range(4)])]
    all_to_all x1, blocking collectives: 52.1 us -> 49.8 us  [shards(): lax.all_to_all(iterate, 'fsdp', split_axis=1, concat_axis=0, tiled=True)]
    dot_general x15, matrix products: 9.65 us -> 7.58 us  [mul(): return jnp.einsum('mij,mjk->mik', a, b, precision=lax.Precision.HIGHEST)]
  transfers between devices with their start and end apart: 1 -> 2, of which waited for: 1 -> 2; matrix products, arithmetic and copies ran while one was open for 0% -> 0% of each run, Pallas kernels for 0% -> 0%
where the time goes in v1:
time: 138 us
  blocking collectives  104 us (75%)
  waiting for transfers between devices  10.3 us (7%)
  matrix products  9.63 us (7%)
  other arithmetic  6.91 us (5%)
  local copies, waits for them, and re-layouts  3.17 us (2%)
  starting transfers between devices  3.14 us (2%)
    all_to_all x1, blocking collectives, shards(): lax.all_to_all(direction, 'fsdp', split_axis=0, concat_axis=1, tiled=True)  54.3 us
    all_to_all x1, blocking collectives, shards(): lax.all_to_all(iterate, 'fsdp', split_axis=1, concat_axis=0, tiled=True)  49.8 us
    ppermute x2, waiting for transfers between devices, shards(): lax.ppermute(gram, 'tp', [(dev, dev ^ hop) for dev in range(4)])  10.3 us
    dot_general x15, matrix products, mul(): return jnp.einsum('mij,mjk->mik', a, b, precision=lax.Precision.HIGHEST)  7.58 us
    add x1, other arithmetic, shards(): direction = hold_rate * new_momentum + gradients  4.27 us
    ppermute x2, starting transfers between devices, shards(): lax.ppermute(gram, 'tp', [(dev, dev ^ hop) for dev in range(4)])  3.14 us
  transfers between devices with their start and end apart: 2, of which 2 were waited for; matrix products, arithmetic and copies ran while one was open for 0% of the time, Pallas kernels for 0%

profile of v1, /device:TPU:0, one launch (start us, length us, event | category | flops | bytes accessed | tf_op | source)
XLA Modules:
  0.0 138.0 jit_solution(11490770226001014746)
XLA Ops:
  0.6 4.3 %multiply_add_fusion = (f32[16,32,1024]{2,1,0:T(8,128)S(1)}, f32[16,32,1024]{2,1,0:T(8,128)}) fusion(f32[16,32,1024]{2,1,0:T(8,128)} %param.3, f32[16,32,1024]{2,1,0:T(8,128)} %param.4), kind=kLoop, calls=%fused_computation.1 | loop fusion | flops 2097152 | bytes 8388608 | tf_op jit(solution)/shard_map/add | solution.py:31
  4.9 54.3 %all_to_all.27 = f32[16,32,1024]{2,1,0:T(8,128)S(1)} all-to-all(f32[16,32,1024]{2,1,0:T(8,128)S(1)} %get-tuple-element.4), channel_id=1, replica_groups=mesh['copy'=2,'fsdp'=4,'tp'=4] {'fsdp'}, dimensions={0} | all-to-all | bytes 4194304 | tf_op jit(solution)/shard_map/all_to_all | solution.py:32
  59.2 0.2 copy.7
  59.5 2.1 %fusion.12 = f32[4,128,128]{2,1,0:T(8,128)S(1)} fusion(f32[4,128,1024]{2,1,0:T(8,128)S(1)} %bitcast.37), kind=kOutput, calls=%fused_computation.25 | convolution fusion | flops 805306368 | bytes 2359296 | tf_op jit(solution)/shard_map/mik,mjk->mij/dot_general | solution.py:33
  61.5 1.6 %collective-permute-start = (f32[4,128,128]{2,1,0:T(8,128)S(1)}, f32[4,128,128]{2,1,0:T(8,128)S(1)}, u32[]{:S(2)}, u32[]{:S(2)}) collective-permute-start(f32[4,128,128]{2,1,0:T(8,128)S(1)} %fusion.12), channel_id=1, source_target_pairs={{0,1},{1,0},{2,3},{3,2},{4,5},{5,4},{6,7},{7,6},{8,9},{9,8},{10,11... | collective-permute-start | bytes 786440 | tf_op jit(solution)/shard_map/ppermute | solution.py:36
  63.1 5.5 %collective-permute-done = f32[4,128,128]{2,1,0:T(8,128)S(1)} collective-permute-done((f32[4,128,128]{2,1,0:T(8,128)S(1)}, f32[4,128,128]{2,1,0:T(8,128)S(1)}, u32[]{:S(2)}, u32[]{:S(2)}) %collective-permute-start) | collective-permute-done | bytes 262176 | tf_op jit(solution)/shard_map/ppermute | solution.py:36
  68.6 1.6 %collective-permute-start.1 = (f32[4,128,128]{2,1,0:T(8,128)S(1)}, f32[4,128,128]{2,1,0:T(8,128)S(1)}, u32[]{:S(2)}, u32[]{:S(2)}) collective-permute-start(f32[4,128,128]{2,1,0:T(8,128)S(1)} %add.34), channel_id=1, source_target_pairs={{0,2},{1,3},{2,0},{3,1},{4,6},{5,7},{6,4},{7,5},{8,10},{9,11},{10,... | collective-permute-start | bytes 786440 | tf_op jit(solution)/shard_map/ppermute | solution.py:36
  70.2 4.8 %collective-permute-done.1 = f32[4,128,128]{2,1,0:T(8,128)S(1)} collective-permute-done((f32[4,128,128]{2,1,0:T(8,128)S(1)}, f32[4,128,128]{2,1,0:T(8,128)S(1)}, u32[]{:S(2)}, u32[]{:S(2)}) %collective-permute-start.1) | collective-permute-done | bytes 262176 | tf_op jit(solution)/shard_map/ppermute | solution.py:36
  75.1 0.1 multiply_reduce_fusion
  75.2 0.5 subtract_add_fusion
  75.7 0.4 fusion.5
  76.1 0.4 fusion.3
  76.6 0.4 fusion.13
  77.0 0.4 fusion.2
  77.4 0.4 fusion.14
  77.8 0.4 fusion.18
  78.2 0.4 fusion.15
  78.6 0.4 fusion.1
  79.0 0.4 fusion.16
  79.4 0.4 fusion.19
  79.8 0.4 fusion.17
  80.2 0.4 fusion
  80.6 0.4 fusion.20
  81.0 1.9 %fusion.21 = f32[4,128,1024]{2,1,0:T(8,128)S(1)} fusion(f32[4,128,128]{2,1,0:T(8,128)S(1)} %fusion.20, f32[4,128,1024]{2,1,0:T(8,128)S(1)} %bitcast.38), kind=kOutput, calls=%fused_computation.34 | convolution fusion | flops 805306368 | bytes 4456448 | tf_op jit(solution)/shard_map/mij,mjk->mik/dot_general | solution.py:13
  82.9 1.4 copy.8
  84.3 49.8 %all_to_all.28 = f32[4,128,1024]{2,0,1:T(4,128)S(1)} all-to-all(f32[4,128,1024]{2,0,1:T(4,128)S(1)} %copy.8), channel_id=1, replica_groups=mesh['copy'=2,'fsdp'=4,'tp'=4] {'fsdp'}, dimensions={1} | all-to-all | bytes 4194304 | tf_op jit(solution)/shard_map/all_to_all | solution.py:38
  134.0 0.7 broadcast_multiply_fusion
  134.7 0.0 copy-start
  134.7 1.2 copy.9
  135.9 0.4 copy-done
  136.3 1.8 %bitcast_subtract_fusion = f32[16,32,1024]{2,1,0:T(8,128)} fusion(f32[4,4,32,1024]{3,2,1,0:T(8,128)S(1)} %copy.9, f32[16,32,1024]{2,1,0:T(8,128)S(1)} %copy-done), kind=kLoop, calls=%fused_computation | loop fusion | flops 1048576 | bytes 6291456 | tf_op jit(solution)/shard_map/sub | solution.py:39
  (4 shorter events, 0.1 us)
Async XLA Ops:
  61.5 7.0 %collective-permute-start = (f32[4,128,128]{2,1,0:T(8,128)S(1)}, f32[4,128,128]{2,1,0:T(8,128)S(1)}, u32[]{:S(2)}, u32[]{:S(2)}) collective-permute-start(f32[4,128,128]{2,1,0:T(8,128)S(1)} %fusion.12), channel_id=1, source_target_pairs={{0,1},{1,0},{2,3},{3,2},{4,5},{5,4},{6,7},{7,6},{8,9},{9,8},{10,11... | collective-permute-start | bytes 786440 | tf_op jit(solution)/shard_map/ppermute | solution.py:36
  68.6 6.4 %collective-permute-start.1 = (f32[4,128,128]{2,1,0:T(8,128)S(1)}, f32[4,128,128]{2,1,0:T(8,128)S(1)}, u32[]{:S(2)}, u32[]{:S(2)}) collective-permute-start(f32[4,128,128]{2,1,0:T(8,128)S(1)} %add.34), channel_id=1, source_target_pairs={{0,2},{1,3},{2,0},{3,1},{4,6},{5,7},{6,4},{7,5},{8,10},{9,11},{10,... | collective-permute-start | bytes 786440 | tf_op jit(solution)/shard_map/ppermute | solution.py:36
  134.7 1.6 %copy-start = (f32[16,32,1024]{2,1,0:T(8,128)S(1)}, f32[16,32,1024]{2,1,0:T(8,128)}, u32[]{:S(2)}) copy-start(f32[16,32,1024]{2,1,0:T(8,128)} %param.5) | copy-start | bytes 6291460
